TPU v7x, 32 devices: a whole 2x2x4 slice. The times are simulated.
32 devices in a mesh: task: 4 (over y, core), param: 8 (over z, x).
Axes of the slice: x: 2, y: 2, z: 4, core: 2. Of those that a mesh axis runs over, the one named last changes fastest.
Arguments:
- params: bfloat16 [16, 512, 4096], P('task', 'param'), may hold values from -6 to 6
- fisher: float32 [16, 512, 4096], P('task', 'param'), may hold values from 3e-06 to 1, as said below
Outputs:
- merged: bfloat16 [512, 4096], P('param')
Inputs may be any that keep to these rules, and one draw needn't show every extreme that they name: `fisher`: every entry is positive; scales differ strongly between tasks and between regions of rows.
All inputs are finite; a program needn't handle non-finite values.
Results may differ from a plain program's by a relative error of at most 0.00045.
Values may be sent and summed in bfloat16 or wider, within the bound.
A program may use at most 64 MiB of HBM per device.

v0:
```python
import jax
import jax.numpy as jnp
from jax import lax
from jax.sharding import PartitionSpec as P


def combined_all(value, axis, join):
    pieces = jax.tree.map(lambda part: lax.all_gather(part, axis), value)
    head = jax.tree.map(lambda part: part[0], pieces)
    tail = jax.tree.map(lambda part: part[1:], pieces)
    total, _ = lax.scan(lambda total, share: (join(total, share), None), head, tail)
    return total


def joined(first, second):
    return (jnp.maximum(first[0], second[0]), first[1] + second[1])


def local(params, fisher):
    local_peak = jnp.max(fisher, axis=(1, 2))
    local_total = jnp.sum(fisher, axis=(1, 2))
    peak, total = combined_all((local_peak, local_total), "param", joined)
    count = float(fisher.shape[1] * lax.axis_size("param") * fisher.shape[2])
    factor = count * peak / total
    weight = jnp.clip(fisher / peak[:, None, None], 0.002, 0.25) * factor[:, None, None]
    numer = jnp.sum(weight * params.astype(jnp.float32), axis=0)
    denom = jnp.sum(weight, axis=0)
    numer, denom = lax.psum((numer, denom), "task")
    return (numer / denom).astype(jnp.bfloat16)


def solution(mesh):
    in_specs = (P("task", "param", None), P("task", "param", None))
    out_specs = P("param", None)
    return jax.shard_map(local, mesh=mesh, in_specs=in_specs, out_specs=out_specs, check_vma=False)
```

profile of v0, /device:TPU:0, one launch (start us, length us, event | category | flops | bytes accessed | tf_op | source)
XLA Modules:
  0.0 97.8 jit_solution(13709745537521834636)
XLA Ops:
  6.5 0.0 copy-start.1
  6.5 0.0 copy-start
  6.5 0.0 all-reduce.6.cloned.1.call-start
  6.5 2.7 %fusion.5 = (f32[4]{0:T(128)S(1)}, f32[4]{0:T(128)S(1)}) fusion(f32[4,64,4096]{2,1,0:T(8,128)} %param.5), kind=kLoop, calls=%fused_computation.11 | loop fusion | flops 2097144 | bytes 4194336 | tf_op jit(solution)/shard_map/reduce_sum | solution.py:21
  9.3 0.0 copy-done.1
  9.3 0.7 dynamic-slice
  10.7 0.2 dynamic-update-slice.1
  10.9 0.2 dynamic-update-slice
  11.1 23.1 %all-reduce.2 = (f32[32]{0:T(128)S(1)}, f32[32]{0:T(128)S(1)}) all-reduce(f32[32]{0:T(128)S(1)} %dynamic-update-slice, f32[32]{0:T(128)S(1)} %dynamic-update-slice.1), channel_id=2, replica_groups=mesh['task'=4,'param'=8] {'param'}, use_global_device_ids=true, to_apply=%add | all-reduce | flops 64 | bytes 512
  34.2 0.1 slice.18
  34.3 0.1 slice.19
  34.4 0.1 reshape.9
  34.4 0.1 reshape.8
  34.5 0.2 while.12
  34.8 0.0 copy-done
  34.8 4.9 %fusion.4 = (f32[64,4096]{1,0:T(8,128)}, f32[64,4096]{1,0:T(8,128)}) fusion(f32[4]{0:T(128)S(1)} %multiply_divide_fusion, f32[4,64,4096]{2,1,0:T(8,128)} %param.5, f32[4]{0:T(128)S(1)} %get-tuple-element.33, bf16[4,64,4096]{2,1,0:T(8,128)(2,1)S(1)} %copy-done), kind=kLoop, calls=%fused_computation.10 | loop fusion | flops 6815744 | bytes 8388640 | tf_op jit(solution)/shard_map/reduce_sum | solution.py:27
  39.7 0.0 all-reduce.6.cloned.1.call-update
  39.7 48.8 %all-reduce.6.cloned.1.call-done = (f32[64,4096]{1,0:T(8,128)}, f32[64,4096]{1,0:T(8,128)}) async-done(((f32[64,4096]{1,0:T(8,128)}, f32[64,4096]{1,0:T(8,128)}), (f32[64,4096]{1,0:T(8,128)}, f32[64,4096]{1,0:T(8,128)})) %all-reduce.6.cloned.1.call-update) | async-done | bytes 2097168 | tf_op jit(solution)/shard_map/psum | solution.py:28
  88.5 2.5 %divide_convert_fusion = bf16[64,4096]{1,0:T(8,128)(2,1)} fusion(f32[64,4096]{1,0:T(8,128)} %get-tuple-element.51, f32[64,4096]{1,0:T(8,128)} %get-tuple-element.52), kind=kLoop, calls=%fused_computation.8 | loop fusion | flops 524288 | bytes 2621440 | tf_op jit(solution)/shard_map/convert_element_type | solution.py:29
  (10 shorter events, 0.1 us)
Async XLA Ops:
  6.5 2.8 %copy-start.1 = (u32[32]{0:T(128)S(1)}, u32[32]{0:T(128)}, u32[]{:S(2)}) copy-start(u32[32]{0:T(128)} %constant.22) | copy-start | bytes 388
  6.5 28.2 %copy-start = (bf16[4,64,4096]{2,1,0:T(8,128)(2,1)S(1)}, bf16[4,64,4096]{2,1,0:T(8,128)(2,1)}, u32[]{:S(2)}) copy-start(bf16[4,64,4096]{2,1,0:T(8,128)(2,1)} %param.4) | copy-start | bytes 6291460
  6.5 82.0 %all-reduce.6.cloned.1.call-start = ((), (), s32[]{:S(2)}) async-start(), calls=%async_computation | async-start | bytes 4194304 | tf_op jit(solution)/shard_map/psum | solution.py:28
Sparse Core Ops, SparseCore 0:
  39.8 48.6 all-reduce.5
where the time goes:
time: 98 us; the launch traced here: 97.8 us
  waiting for transfers between devices  48.8 us (50%)
  blocking collectives  23.1 us (24%)
  between operations  14.1 us (14%)
  other arithmetic  10.2 us (10%)
  local copies, waits for them, and re-layouts  1.43 us (1%)
    psum x1, waiting for transfers between devices, local(): numer, denom = lax.psum((numer, denom), 'task')  48.8 us
    unnamed x1, blocking collectives  23.1 us
    reduce_sum x1, other arithmetic, local(): denom = jnp.sum(weight, axis=0)  4.9 us
    reduce_sum x1, other arithmetic, local(): local_total = jnp.sum(fisher, axis=(1, 2))  2.75 us
    convert_element_type x1, other arithmetic, local(): return (numer / denom).astype(jnp.bfloat16)  2.48 us
  transfers between devices with their start and end apart: 1, of which 1 were waited for; matrix products, arithmetic and copies ran while one was open for 0% of the time, Pallas kernels for 0%

commit v1 on v0

v1 whole, which is shorter than its diff:
```python
import functools

import jax
import jax.numpy as jnp
from jax import lax
from jax.experimental import pallas as pl
from jax.experimental.pallas import tpu as pltpu
from jax.sharding import PartitionSpec as P

MESH = pl.DeviceIdType.MESH
LANES = 128
PIECES = 8


def kernel(tasks, groups, params_hbm, fisher_hbm, out, fisher, params, stats, give, take, bound, kept, landed,
           load_f, load_p, stat_send, stat_recv, give_send, give_recv, y_send, y_recv, res_send, res_recv,
           near_send, near_recv):
    count, rows, width = fisher.shape
    chips = tasks // 2
    chunks, chunk = give.shape[2], give.shape[5]
    half, piece = width // 2, width // tasks
    task, param = lax.axis_index("task"), lax.axis_index("param")
    chip, core = task // 2, task % 2
    partner = {"task": chip * 2 + 1 - core, "param": param}

    def chip_at(shift):
        return lax.rem(chip + shift, chips)

    def same_core(shift):
        return {"task": chip_at(shift) * 2 + core, "param": param}

    def member(shift):
        return {"task": task, "param": lax.rem(param + shift, groups)}

    loads_f = [pltpu.make_async_copy(fisher_hbm.at[t], fisher.at[t], load_f.at[t]) for t in range(count)]
    loads_p = [pltpu.make_async_copy(params_hbm.at[t], params.at[t], load_p.at[t]) for t in range(count)]
    for copy in loads_f + loads_p:
        copy.start()

    barrier = pltpu.get_barrier_semaphore()
    greeted = [member(s) for s in range(1, groups)] + [partner] + [same_core(s) for s in range(1, chips)]
    for device in greeted:
        pl.semaphore_signal(barrier, inc=1, device_id=device, device_id_type=MESH)

    tops, sums = [], []
    for t in range(count):
        loads_f[t].wait()

        def over(step, carry, t=t):
            block = fisher[t, :, pl.ds(pl.multiple_of(step * LANES, LANES), LANES)]
            return jnp.maximum(carry[0], block), carry[1] + block

        first = fisher[t, :, 0:LANES]
        top, total = lax.fori_loop(1, width // LANES, over, (first, first), unroll=8)
        tops.append(jnp.max(top, axis=0, keepdims=True))
        sums.append(jnp.sum(total, axis=0, keepdims=True))
    top = jnp.max(jnp.concatenate(tops, axis=0), axis=1, keepdims=True)
    total = jnp.sum(jnp.concatenate(sums, axis=0), axis=1, keepdims=True)
    stats[0, 0:count, :] = jnp.broadcast_to(top, (count, LANES))
    stats[0, count:2 * count, :] = jnp.broadcast_to(total, (count, LANES))

    pl.semaphore_wait(barrier, len(greeted))

    stat_copies = [
        pltpu.make_async_remote_copy(
            src_ref=stats.at[0], dst_ref=stats.at[s], send_sem=stat_send.at[s], recv_sem=stat_recv.at[s],
            device_id=member(s), device_id_type=MESH)
        for s in range(1, groups)
    ]
    for copy in stat_copies:
        copy.start()
    for copy in loads_p:
        copy.wait()
    for copy in stat_copies:
        copy.wait_recv()
    peak, total = stats[0, 0:count, :], stats[0, count:2 * count, :]
    for s in range(1, groups):
        peak = jnp.maximum(peak, stats[s, 0:count, :])
        total = total + stats[s, count:2 * count, :]
    size = float(rows * groups * width)
    gain = size / total
    factor = peak * gain
    low, high = 0.002 * factor, 0.25 * factor
    spread = [
        tuple(jnp.broadcast_to(a[t:t + 1, :], (rows, LANES)) for a in (gain, low, high)) for t in range(count)
    ]

    def partial(side, target, k):
        numers, denoms = [], []
        for part in range(chunk // LANES):
            start = pl.multiple_of(side * half + target * piece + k * chunk + part * LANES, LANES)
            numer = denom = None
            for t in range(count):
                gain_t, low_t, high_t = spread[t]
                info = fisher[t, :, pl.ds(start, LANES)]
                theta = params[t, :, pl.ds(start, LANES)].astype(jnp.float32)
                weight = jnp.minimum(jnp.maximum(info * gain_t, low_t), high_t)
                numer = weight * theta if t == 0 else numer + weight * theta
                denom = weight if t == 0 else denom + weight
            numers.append(numer)
            denoms.append(denom)
        if len(numers) == 1:
            return numers[0], denoms[0]
        return jnp.concatenate(numers, axis=1), jnp.concatenate(denoms, axis=1)

    def put(ref, pair):
        ref[0], ref[1] = pair

    def added(one, two):
        return one[0] + two[0], one[1] + two[1]

    def give_copy(shift, k):
        return pltpu.make_async_remote_copy(
            src_ref=give.at[shift, 0, k], dst_ref=take.at[shift, 0, k], send_sem=give_send.at[shift, k],
            recv_sem=give_recv.at[shift, k], device_id=partner, device_id_type=MESH)

    def y_copy(shift, k):
        return pltpu.make_async_remote_copy(
            src_ref=bound.at[shift - 1, k], dst_ref=landed.at[shift - 1, k], send_sem=y_send.at[shift - 1, k],
            recv_sem=y_recv.at[shift - 1, k], device_id=same_core(shift), device_id_type=MESH)

    def columns(side, target, k):
        return pl.ds(pl.multiple_of(side * half + target * piece + k * chunk, LANES), chunk)

    def res_copy(shift, k):
        where = out.at[:, columns(core, chip, k)]
        return pltpu.make_async_remote_copy(
            src_ref=where, dst_ref=where, send_sem=res_send.at[shift - 1, k], recv_sem=res_recv.at[shift - 1, k],
            device_id=same_core(shift), device_id_type=MESH)

    def near_copy(shift, k):
        where = out.at[:, columns(core, chip_at(chips - shift), k)]
        return pltpu.make_async_remote_copy(
            src_ref=where, dst_ref=where, send_sem=near_send.at[shift, k], recv_sem=near_recv.at[shift, k],
            device_id=partner, device_id_type=MESH)

    away = [(shift, k) for k in range(chunks) for shift in range(1, chips)]
    gives = {}

    def hand_over(shift, k):
        put(give.at[shift, 0, k], partial(1 - core, chip_at(shift), k))
        gives[shift, k] = give_copy(shift, k)
        gives[shift, k].start()

    for shift, k in away:
        hand_over(shift, k)
    for shift, k in away:
        put(bound.at[shift - 1, k], partial(core, chip_at(shift), k))
    y_copies = {}
    for shift, k in away:
        gives[shift, k].wait_recv()
        put(bound.at[shift - 1, k], added(bound.at[shift - 1, k], take.at[shift, 0, k]))
        y_copies[shift, k] = y_copy(shift, k)
        y_copies[shift, k].start()
    for k in range(chunks):
        hand_over(0, k)
    for k in range(chunks):
        put(kept.at[k], partial(core, chip, k))
    for k in range(chunks):
        gives[0, k].wait_recv()
        put(kept.at[k], added(kept.at[k], take.at[0, 0, k]))

    res_copies, near_copies = {}, {}
    for k in range(chunks):
        total = kept[k, 0], kept[k, 1]
        for shift in range(1, chips):
            y_copies[shift, k].wait_recv()
            total = added(total, landed.at[shift - 1, k])
        out[:, columns(core, chip, k)] = (total[0] / total[1]).astype(out.dtype)
        for shift in range(1, chips):
            res_copies[shift, k] = res_copy(shift, k)
            res_copies[shift, k].start()
        near_copies[0, k] = near_copy(0, k)
        near_copies[0, k].start()
    for shift, k in away:
        res_copies[shift, k].wait_recv()
        near_copies[shift, k] = near_copy(shift, k)
        near_copies[shift, k].start()
    for copies in (gives, y_copies, res_copies):
        for copy in copies.values():
            copy.wait_send()
    for copy in stat_copies:
        copy.wait_send()
    for copy in near_copies.values():
        copy.wait()


def local(mesh, params, fisher):
    count, rows, width = fisher.shape
    tasks, groups = mesh.shape["task"], mesh.shape["param"]
    chips, piece = tasks // 2, width // tasks
    chunks = max(1, min(PIECES, piece // LANES))
    chunk = piece // chunks
    far = max(1, chips - 1)
    f32, dma = jnp.float32, pltpu.SemaphoreType.DMA
    return pl.pallas_call(
        functools.partial(kernel, tasks, groups),
        out_shape=pltpu.VMEM((rows, width), jnp.bfloat16),
        in_specs=[pl.BlockSpec(memory_space=pltpu.HBM)] * 2,
        out_specs=pl.BlockSpec(memory_space=pltpu.VMEM),
        scratch_shapes=[
            pltpu.VMEM((count, rows, width), f32),
            pltpu.VMEM((count, rows, width), jnp.bfloat16),
            pltpu.VMEM((groups, 2 * count, LANES), f32),
            pltpu.VMEM((chips, 1, chunks, 2, rows, chunk), f32),
            pltpu.VMEM((chips, 1, chunks, 2, rows, chunk), f32),
            pltpu.VMEM((far, chunks, 2, rows, chunk), f32),
            pltpu.VMEM((chunks, 2, rows, chunk), f32),
            pltpu.VMEM((far, chunks, 2, rows, chunk), f32),
            dma((count,)),
            dma((count,)),
            dma((groups,)),
            dma((groups,)),
            dma((chips, chunks)),
            dma((chips, chunks)),
            dma((far, chunks)),
            dma((far, chunks)),
            dma((far, chunks)),
            dma((far, chunks)),
            dma((chips, chunks)),
            dma((chips, chunks)),
        ],
        compiler_params=pltpu.CompilerParams(collective_id=0, has_side_effects=True),
        name="merge",
    )(params, fisher)


def solution(mesh):
    in_specs = (P("task", "param", None), P("task", "param", None))
    out_specs = P("param", None)
    return jax.shard_map(
        functools.partial(local, mesh), mesh=mesh, in_specs=in_specs, out_specs=out_specs, check_vma=False)
```

time: 98 us -> 31.1 us (0.32)
  waiting for transfers between devices: 48.8 us -> 0 us
  Pallas kernels: 0 us -> 30.1 us
  blocking collectives: 23.1 us -> 0 us
  between operations: 14.1 us -> 0.01 us
  other arithmetic: 10.2 us -> 0 us
    psum x1 -> x0, waiting for transfers between devices: 48.8 us -> none  [local(): numer, denom = lax.psum((numer, denom), 'task')]
    pallas_call x0 -> x1, Pallas kernels: none -> 30.1 us  [local(): pl.pallas_call(functools.partial(kernel, tasks, groups), out_shape=pltpu....]
    unnamed x1 -> x0, blocking collectives: 23.1 us -> none
    reduce_sum x2 -> x0, other arithmetic: 7.65 us -> none  [the longest x1 4.9 us: local(): denom = jnp.sum(weight, axis=0)]
    convert_element_type x1 -> x0, other arithmetic: 2.48 us -> none  [local(): return (numer / denom).astype(jnp.bfloat16)]
  transfers between devices with their start and end apart: 1 -> 0, of which waited for: 1 -> 0; matrix products, arithmetic and copies ran while one was open for 0% -> 0% of each run, Pallas kernels for 0% -> 0%
where the time goes in v1:
time: 31.1 us; the launch traced here: 30.9 us
  Pallas kernels  30.1 us (97%)
  local copies, waits for them, and re-layouts  0.8 us (3%)
    pallas_call x1, Pallas kernels, local(): pl.pallas_call(functools.partial(kernel, tasks, groups), out_shape=pltpu....  30.1 us
    unnamed x1, local copies, waits for them, and re-layouts  0.8 us

profile of v1, /device:TPU:0, one launch (start us, length us, event | category | flops | bytes accessed | tf_op | source)
XLA Modules:
  0.0 30.9 jit_solution(12708952533346922127)
XLA Ops:
  0.0 30.1 %merge.1 = bf16[64,4096]{1,0:T(8,128)(2,1)S(1)} custom-call(bf16[4,64,4096]{2,1,0:T(8,128)(2,1)} %params_hbm.1, f32[4,64,4096]{2,1,0:T(8,128)} %fisher_hbm.1), custom_call_target="tpu_custom_call" | custom-call | tf_op jit(solution)/shard_map/merge/pallas_call | solution.py:196
  30.1 0.8 %copy.4 = bf16[64,4096]{1,0:T(8,128)(2,1)} copy(bf16[64,4096]{1,0:T(8,128)(2,1)S(1)} %merge.1) | data formatting | bytes 1048576

commit v2 on v1

--- a/solution.py
+++ b/solution.py
@@ -12,9 +12,33 @@
 PIECES = 8
 
 
-def kernel(tasks, groups, params_hbm, fisher_hbm, out, fisher, params, stats, give, take, bound, kept, landed,
-           load_f, load_p, stat_send, stat_recv, give_send, give_recv, y_send, y_recv, res_send, res_recv,
-           near_send, near_recv):
+def split(value):
+    scaled = value * 257.0
+    kept = scaled - (scaled - value)
+    low = kept * 0.74
+    scaled = low * 8388609.0
+    return kept, scaled - (scaled - low)
+
+
+def coded(numer, denom):
+    top = numer.astype(jnp.bfloat16)
+    wide = top.astype(jnp.float32)
+    rest = (numer - wide) / jnp.where(wide == 0.0, 1.0, wide)
+    rest = jnp.clip(jnp.round(rest * 32768.0), -127.0, 127.0)
+    kept, power = split(denom)
+    return kept + rest * (power * (1.0 / 8388608.0)), top
+
+
+def decoded(carrier, top):
+    kept, power = split(carrier)
+    wide = top.astype(jnp.float32)
+    return wide + wide * ((carrier - kept) / power * 256.0), kept
+
+
+def kernel(tasks, groups, params_hbm, fisher_hbm, out, fisher, params, stats, give, take, bound, kept,
+           wide_out, top_out, wide_in, top_in,
+           load_f, load_p, stat_send, stat_recv, give_send, give_recv, y_send, y_recv, top_send, top_recv,
+           res_send, res_recv, near_send, near_recv):
     count, rows, width = fisher.shape
     chips = tasks // 2
     chunks, chunk = give.shape[2], give.shape[5]
@@ -34,7 +58,7 @@
 
     loads_f = [pltpu.make_async_copy(fisher_hbm.at[t], fisher.at[t], load_f.at[t]) for t in range(count)]
     loads_p = [pltpu.make_async_copy(params_hbm.at[t], params.at[t], load_p.at[t]) for t in range(count)]
-    for copy in loads_f + loads_p:
+    for copy in loads_f:
         copy.start()
 
     barrier = pltpu.get_barrier_semaphore()
@@ -45,6 +69,9 @@
     tops, sums = [], []
     for t in range(count):
         loads_f[t].wait()
+        if t == count - 1:
+            for copy in loads_p:
+                copy.start()
 
         def over(step, carry, t=t):
             block = fisher[t, :, pl.ds(pl.multiple_of(step * LANES, LANES), LANES)]
@@ -115,9 +142,13 @@
             recv_sem=give_recv.at[shift, k], device_id=partner, device_id_type=MESH)
 
     def y_copy(shift, k):
-        return pltpu.make_async_remote_copy(
-            src_ref=bound.at[shift - 1, k], dst_ref=landed.at[shift - 1, k], send_sem=y_send.at[shift - 1, k],
-            recv_sem=y_recv.at[shift - 1, k], device_id=same_core(shift), device_id_type=MESH)
+        return [
+            pltpu.make_async_remote_copy(
+                src_ref=source.at[shift - 1, k], dst_ref=sink.at[shift - 1, k], send_sem=send.at[shift - 1, k],
+                recv_sem=recv.at[shift - 1, k], device_id=same_core(shift), device_id_type=MESH)
+            for source, sink, send, recv in (
+                (wide_out, wide_in, y_send, y_recv), (top_out, top_in, top_send, top_recv))
+        ]
 
     def columns(side, target, k):
         return pl.ds(pl.multiple_of(side * half + target * piece + k * chunk, LANES), chunk)
@@ -149,9 +180,11 @@
     y_copies = {}
     for shift, k in away:
         gives[shift, k].wait_recv()
-        put(bound.at[shift - 1, k], added(bound.at[shift - 1, k], take.at[shift, 0, k]))
+        wide_out[shift - 1, k], top_out[shift - 1, k] = coded(
+            *added(bound.at[shift - 1, k], take.at[shift, 0, k]))
         y_copies[shift, k] = y_copy(shift, k)
-        y_copies[shift, k].start()
+        for copy in y_copies[shift, k]:
+            copy.start()
     for k in range(chunks):
         hand_over(0, k)
     for k in range(chunks):
@@ -164,8 +197,9 @@
     for k in range(chunks):
         total = kept[k, 0], kept[k, 1]
         for shift in range(1, chips):
-            y_copies[shift, k].wait_recv()
-            total = added(total, landed.at[shift - 1, k])
+            for copy in y_copies[shift, k]:
+                copy.wait_recv()
+            total = added(total, decoded(wide_in[shift - 1, k], top_in[shift - 1, k]))
         out[:, columns(core, chip, k)] = (total[0] / total[1]).astype(out.dtype)
         for shift in range(1, chips):
             res_copies[shift, k] = res_copy(shift, k)
@@ -176,8 +210,11 @@
         res_copies[shift, k].wait_recv()
         near_copies[shift, k] = near_copy(shift, k)
         near_copies[shift, k].start()
-    for copies in (gives, y_copies, res_copies):
+    for copies in (gives, res_copies):
         for copy in copies.values():
+            copy.wait_send()
+    for pair in y_copies.values():
+        for copy in pair:
             copy.wait_send()
     for copy in stat_copies:
         copy.wait_send()
@@ -206,13 +243,18 @@
             pltpu.VMEM((chips, 1, chunks, 2, rows, chunk), f32),
             pltpu.VMEM((far, chunks, 2, rows, chunk), f32),
             pltpu.VMEM((chunks, 2, rows, chunk), f32),
-            pltpu.VMEM((far, chunks, 2, rows, chunk), f32),
+            pltpu.VMEM((far, chunks, rows, chunk), f32),
+            pltpu.VMEM((far, chunks, rows, chunk), jnp.bfloat16),
+            pltpu.VMEM((far, chunks, rows, chunk), f32),
+            pltpu.VMEM((far, chunks, rows, chunk), jnp.bfloat16),
             dma((count,)),
             dma((count,)),
             dma((groups,)),
             dma((groups,)),
             dma((chips, chunks)),
             dma((chips, chunks)),
+            dma((far, chunks)),
+            dma((far, chunks)),
             dma((far, chunks)),
             dma((far, chunks)),
             dma((far, chunks)),

time: 31.1 us -> 28 us (0.900)
  Pallas kernels: 30.1 us -> 27 us
    pallas_call x1, Pallas kernels: 30.1 us -> 27 us  [local(): pl.pallas_call(functools.partial(kernel, tasks, groups), out_shape=pltpu....]
where the time goes in v2:
time: 28 us; the launch traced here: 27.8 us
  Pallas kernels  27 us (96%)
  local copies, waits for them, and re-layouts  0.8 us (3%)
    pallas_call x1, Pallas kernels, local(): pl.pallas_call(functools.partial(kernel, tasks, groups), out_shape=pltpu....  27 us
    unnamed x1, local copies, waits for them, and re-layouts  0.8 us

profile of v2, /device:TPU:0, one launch (start us, length us, event | category | flops | bytes accessed | tf_op | source)
XLA Modules:
  0.0 27.8 jit_solution(3286877761144607989)
XLA Ops:
  0.0 27.0 %merge.1 = bf16[64,4096]{1,0:T(8,128)(2,1)S(1)} custom-call(bf16[4,64,4096]{2,1,0:T(8,128)(2,1)} %params_hbm.1, f32[4,64,4096]{2,1,0:T(8,128)} %fisher_hbm.1), custom_call_target="tpu_custom_call" | custom-call | tf_op jit(solution)/shard_map/merge/pallas_call | solution.py:233
  27.0 0.8 %copy.4 = bf16[64,4096]{1,0:T(8,128)(2,1)} copy(bf16[64,4096]{1,0:T(8,128)(2,1)S(1)} %merge.1) | data formatting | bytes 1048576

commit v3 on v2

--- a/solution.py
+++ b/solution.py
@@ -35,10 +35,10 @@
     return wide + wide * ((carrier - kept) / power * 256.0), kept
 
 
-def kernel(tasks, groups, params_hbm, fisher_hbm, out, fisher, params, stats, give, take, bound, kept,
+def kernel(tasks, groups, params_hbm, fisher_hbm, out, fisher, params, stats, give, take, kept,
            wide_out, top_out, wide_in, top_in,
            load_f, load_p, stat_send, stat_recv, give_send, give_recv, y_send, y_recv, top_send, top_recv,
-           res_send, res_recv, near_send, near_recv):
+           res_send, res_recv, cross_send, cross_recv, near_send, near_recv):
     count, rows, width = fisher.shape
     chips = tasks // 2
     chunks, chunk = give.shape[2], give.shape[5]
@@ -62,7 +62,9 @@
         copy.start()
 
     barrier = pltpu.get_barrier_semaphore()
-    greeted = [member(s) for s in range(1, groups)] + [partner] + [same_core(s) for s in range(1, chips)]
+    greeted = [member(s) for s in range(1, groups)] + [partner]
+    for s in range(1, chips):
+        greeted += [same_core(s), {"task": chip_at(s) * 2 + 1 - core, "param": param}]
     for device in greeted:
         pl.semaphore_signal(barrier, inc=1, device_id=device, device_id_type=MESH)
 
@@ -83,8 +85,10 @@
         sums.append(jnp.sum(total, axis=0, keepdims=True))
     top = jnp.max(jnp.concatenate(tops, axis=0), axis=1, keepdims=True)
     total = jnp.sum(jnp.concatenate(sums, axis=0), axis=1, keepdims=True)
-    stats[0, 0:count, :] = jnp.broadcast_to(top, (count, LANES))
-    stats[0, count:2 * count, :] = jnp.broadcast_to(total, (count, LANES))
+    both = jnp.broadcast_to(jnp.concatenate([top, total], axis=0), (2 * count, LANES))
+    lane = lax.broadcasted_iota(jnp.int32, both.shape, 1)
+    own_lane = lane == lax.broadcasted_iota(jnp.int32, both.shape, 0)
+    stats[0] = jnp.sum(jnp.where(own_lane, both, 0.0), axis=0, keepdims=True)
 
     pl.semaphore_wait(barrier, len(greeted))
 
@@ -100,17 +104,16 @@
         copy.wait()
     for copy in stat_copies:
         copy.wait_recv()
-    peak, total = stats[0, 0:count, :], stats[0, count:2 * count, :]
+    peak = total = stats[0]
     for s in range(1, groups):
-        peak = jnp.maximum(peak, stats[s, 0:count, :])
-        total = total + stats[s, count:2 * count, :]
+        peak = jnp.maximum(peak, stats[s])
+        total = total + stats[s]
     size = float(rows * groups * width)
-    gain = size / total
-    factor = peak * gain
-    low, high = 0.002 * factor, 0.25 * factor
-    spread = [
-        tuple(jnp.broadcast_to(a[t:t + 1, :], (rows, LANES)) for a in (gain, low, high)) for t in range(count)
-    ]
+    spread = []
+    for t in range(count):
+        gain = size / jnp.broadcast_to(total[:, count + t:count + t + 1], (1, LANES))
+        factor = jnp.broadcast_to(peak[:, t:t + 1], (1, LANES)) * gain
+        spread.append([jnp.broadcast_to(a, (rows, LANES)) for a in (gain, 0.002 * factor, 0.25 * factor)])
 
     def partial(side, target, k):
         numers, denoms = [], []
@@ -159,6 +162,12 @@
             src_ref=where, dst_ref=where, send_sem=res_send.at[shift - 1, k], recv_sem=res_recv.at[shift - 1, k],
             device_id=same_core(shift), device_id_type=MESH)
 
+    def cross_copy(shift):
+        where = out.at[:, columns(core, chip, chunks - 1)]
+        return pltpu.make_async_remote_copy(
+            src_ref=where, dst_ref=where, send_sem=cross_send.at[shift - 1], recv_sem=cross_recv.at[shift - 1],
+            device_id={"task": chip_at(shift) * 2 + 1 - core, "param": param}, device_id_type=MESH)
+
     def near_copy(shift, k):
         where = out.at[:, columns(core, chip_at(chips - shift), k)]
         return pltpu.make_async_remote_copy(
@@ -175,23 +184,20 @@
 
     for shift, k in away:
         hand_over(shift, k)
-    for shift, k in away:
-        put(bound.at[shift - 1, k], partial(core, chip_at(shift), k))
     y_copies = {}
     for shift, k in away:
+        own = partial(core, chip_at(shift), k)
         gives[shift, k].wait_recv()
-        wide_out[shift - 1, k], top_out[shift - 1, k] = coded(
-            *added(bound.at[shift - 1, k], take.at[shift, 0, k]))
+        wide_out[shift - 1, k], top_out[shift - 1, k] = coded(*added(own, take.at[shift, 0, k]))
         y_copies[shift, k] = y_copy(shift, k)
         for copy in y_copies[shift, k]:
             copy.start()
     for k in range(chunks):
         hand_over(0, k)
     for k in range(chunks):
-        put(kept.at[k], partial(core, chip, k))
-    for k in range(chunks):
+        own = partial(core, chip, k)
         gives[0, k].wait_recv()
-        put(kept.at[k], added(kept.at[k], take.at[0, 0, k]))
+        put(kept.at[k], added(own, take.at[0, 0, k]))
 
     res_copies, near_copies = {}, {}
     for k in range(chunks):
@@ -206,10 +212,16 @@
             res_copies[shift, k].start()
         near_copies[0, k] = near_copy(0, k)
         near_copies[0, k].start()
+    crosses = [cross_copy(shift) for shift in range(1, chips)]
+    for copy in crosses:
+        copy.start()
     for shift, k in away:
         res_copies[shift, k].wait_recv()
-        near_copies[shift, k] = near_copy(shift, k)
-        near_copies[shift, k].start()
+        if k < chunks - 1:
+            near_copies[shift, k] = near_copy(shift, k)
+            near_copies[shift, k].start()
+    for copy in crosses:
+        copy.wait()
     for copies in (gives, res_copies):
         for copy in copies.values():
             copy.wait_send()
@@ -238,10 +250,9 @@
         scratch_shapes=[
             pltpu.VMEM((count, rows, width), f32),
             pltpu.VMEM((count, rows, width), jnp.bfloat16),
-            pltpu.VMEM((groups, 2 * count, LANES), f32),
+            pltpu.VMEM((groups, 1, LANES), f32),
             pltpu.VMEM((chips, 1, chunks, 2, rows, chunk), f32),
             pltpu.VMEM((chips, 1, chunks, 2, rows, chunk), f32),
-            pltpu.VMEM((far, chunks, 2, rows, chunk), f32),
             pltpu.VMEM((chunks, 2, rows, chunk), f32),
             pltpu.VMEM((far, chunks, rows, chunk), f32),
             pltpu.VMEM((far, chunks, rows, chunk), jnp.bfloat16),
@@ -259,6 +270,8 @@
             dma((far, chunks)),
             dma((far, chunks)),
             dma((far, chunks)),
+            dma((far,)),
+            dma((far,)),
             dma((chips, chunks)),
             dma((chips, chunks)),
         ],

time: 28 us -> 27.7 us (0.989)
  Pallas kernels: 27 us -> 26.7 us
where the time goes in v3:
time: 27.7 us; the launch traced here: 27.5 us
  Pallas kernels  26.7 us (96%)
  local copies, waits for them, and re-layouts  0.8 us (3%)
    pallas_call x1, Pallas kernels, local(): pl.pallas_call(functools.partial(kernel, tasks, groups), out_shape=pltpu....  26.7 us
    unnamed x1, local copies, waits for them, and re-layouts  0.8 us

profile of v3, /device:TPU:0, one launch (start us, length us, event | category | flops | bytes accessed | tf_op | source)
XLA Modules:
  0.0 27.5 jit_solution(14151208110607156963)
XLA Ops:
  0.0 26.7 %merge.1 = bf16[64,4096]{1,0:T(8,128)(2,1)S(1)} custom-call(bf16[4,64,4096]{2,1,0:T(8,128)(2,1)} %params_hbm.1, f32[4,64,4096]{2,1,0:T(8,128)} %fisher_hbm.1), custom_call_target="tpu_custom_call" | custom-call | tf_op jit(solution)/shard_map/merge/pallas_call | solution.py:245
  26.8 0.8 %copy.4 = bf16[64,4096]{1,0:T(8,128)(2,1)} copy(bf16[64,4096]{1,0:T(8,128)(2,1)S(1)} %merge.1) | data formatting | bytes 1048576

commit v4 on v3

--- a/solution.py
+++ b/solution.py
@@ -37,7 +37,7 @@
 
 def kernel(tasks, groups, params_hbm, fisher_hbm, out, fisher, params, stats, give, take, kept,
            wide_out, top_out, wide_in, top_in,
-           load_f, load_p, stat_send, stat_recv, give_send, give_recv, y_send, y_recv, top_send, top_recv,
+           load_f, load_p, stat_send, stat_recv, give_send, give_recv, kept_recv, y_send, y_recv, top_send, top_recv,
            res_send, res_recv, cross_send, cross_recv, near_send, near_recv):
     count, rows, width = fisher.shape
     chips = tasks // 2
@@ -56,8 +56,11 @@
     def member(shift):
         return {"task": task, "param": lax.rem(param + shift, groups)}
 
+    def drain(ref, semaphore):
+        pltpu.make_async_copy(ref, ref, semaphore).wait()
+
     loads_f = [pltpu.make_async_copy(fisher_hbm.at[t], fisher.at[t], load_f.at[t]) for t in range(count)]
-    loads_p = [pltpu.make_async_copy(params_hbm.at[t], params.at[t], load_p.at[t]) for t in range(count)]
+    loads_p = [pltpu.make_async_copy(params_hbm.at[t], params.at[t], load_p) for t in range(count)]
     for copy in loads_f:
         copy.start()
 
@@ -94,16 +97,14 @@
 
     stat_copies = [
         pltpu.make_async_remote_copy(
-            src_ref=stats.at[0], dst_ref=stats.at[s], send_sem=stat_send.at[s], recv_sem=stat_recv.at[s],
+            src_ref=stats.at[0], dst_ref=stats.at[s], send_sem=stat_send, recv_sem=stat_recv,
             device_id=member(s), device_id_type=MESH)
         for s in range(1, groups)
     ]
     for copy in stat_copies:
         copy.start()
-    for copy in loads_p:
-        copy.wait()
-    for copy in stat_copies:
-        copy.wait_recv()
+    drain(params, load_p)
+    drain(stats.at[1:groups], stat_recv)
     peak = total = stats[0]
     for s in range(1, groups):
         peak = jnp.maximum(peak, stats[s])
@@ -141,13 +142,13 @@
 
     def give_copy(shift, k):
         return pltpu.make_async_remote_copy(
-            src_ref=give.at[shift, 0, k], dst_ref=take.at[shift, 0, k], send_sem=give_send.at[shift, k],
-            recv_sem=give_recv.at[shift, k], device_id=partner, device_id_type=MESH)
+            src_ref=give.at[shift, 0, k], dst_ref=take.at[shift, 0, k], send_sem=give_send,
+            recv_sem=give_recv.at[shift - 1, k] if shift else kept_recv, device_id=partner, device_id_type=MESH)
 
     def y_copy(shift, k):
         return [
             pltpu.make_async_remote_copy(
-                src_ref=source.at[shift - 1, k], dst_ref=sink.at[shift - 1, k], send_sem=send.at[shift - 1, k],
+                src_ref=source.at[shift - 1, k], dst_ref=sink.at[shift - 1, k], send_sem=send,
                 recv_sem=recv.at[shift - 1, k], device_id=same_core(shift), device_id_type=MESH)
             for source, sink, send, recv in (
                 (wide_out, wide_in, y_send, y_recv), (top_out, top_in, top_send, top_recv))
@@ -159,7 +160,7 @@
     def res_copy(shift, k):
         where = out.at[:, columns(core, chip, k)]
         return pltpu.make_async_remote_copy(
-            src_ref=where, dst_ref=where, send_sem=res_send.at[shift - 1, k], recv_sem=res_recv.at[shift - 1, k],
+            src_ref=where, dst_ref=where, send_sem=res_send.at[shift - 1], recv_sem=res_recv.at[shift - 1, k],
             device_id=same_core(shift), device_id_type=MESH)
 
     def cross_copy(shift):
@@ -171,7 +172,7 @@
     def near_copy(shift, k):
         where = out.at[:, columns(core, chip_at(chips - shift), k)]
         return pltpu.make_async_remote_copy(
-            src_ref=where, dst_ref=where, send_sem=near_send.at[shift, k], recv_sem=near_recv.at[shift, k],
+            src_ref=where, dst_ref=where, send_sem=near_send.at[shift], recv_sem=near_recv.at[shift],
             device_id=partner, device_id_type=MESH)
 
     away = [(shift, k) for k in range(chunks) for shift in range(1, chips)]
@@ -195,13 +196,12 @@
     for k in range(chunks):
         hand_over(0, k)
     for k in range(chunks):
-        own = partial(core, chip, k)
-        gives[0, k].wait_recv()
-        put(kept.at[k], added(own, take.at[0, 0, k]))
+        put(kept.at[k], partial(core, chip, k))
+    drain(take.at[0], kept_recv)
 
     res_copies, near_copies = {}, {}
     for k in range(chunks):
-        total = kept[k, 0], kept[k, 1]
+        total = added(kept.at[k], take.at[0, 0, k])
         for shift in range(1, chips):
             for copy in y_copies[shift, k]:
                 copy.wait_recv()
@@ -222,16 +222,17 @@
             near_copies[shift, k].start()
     for copy in crosses:
         copy.wait()
-    for copies in (gives, res_copies):
-        for copy in copies.values():
-            copy.wait_send()
-    for pair in y_copies.values():
-        for copy in pair:
-            copy.wait_send()
-    for copy in stat_copies:
-        copy.wait_send()
-    for copy in near_copies.values():
-        copy.wait()
+    drain(stats.at[1:groups], stat_send)
+    drain(give, give_send)
+    drain(wide_out, y_send)
+    drain(top_out, top_send)
+    for shift in range(chips):
+        passed = out.at[:, 0:piece - chunk if shift else piece]
+        if shift:
+            drain(out.at[:, 0:piece], res_send.at[shift - 1])
+        if chunks > 1 or not shift:
+            drain(passed, near_send.at[shift])
+            drain(passed, near_recv.at[shift])
 
 
 def local(mesh, params, fisher):
@@ -259,21 +260,22 @@
             pltpu.VMEM((far, chunks, rows, chunk), f32),
             pltpu.VMEM((far, chunks, rows, chunk), jnp.bfloat16),
             dma((count,)),
-            dma((count,)),
-            dma((groups,)),
-            dma((groups,)),
-            dma((chips, chunks)),
-            dma((chips, chunks)),
-            dma((far, chunks)),
-            dma((far, chunks)),
-            dma((far, chunks)),
-            dma((far, chunks)),
-            dma((far, chunks)),
+            dma,
+            dma,
+            dma,
+            dma,
+            dma((far, chunks)),
+            dma,
+            dma,
+            dma((far, chunks)),
+            dma,
+            dma((far, chunks)),
+            dma((far,)),
             dma((far, chunks)),
             dma((far,)),
             dma((far,)),
-            dma((chips, chunks)),
-            dma((chips, chunks)),
+            dma((chips,)),
+            dma((chips,)),
         ],
         compiler_params=pltpu.CompilerParams(collective_id=0, has_side_effects=True),
         name="merge",

time: 27.7 us -> 26.9 us (0.971)
  Pallas kernels: 26.7 us -> 25.9 us
    pallas_call x1, Pallas kernels: 26.7 us -> 25.9 us  [local(): pl.pallas_call(functools.partial(kernel, tasks, groups), out_shape=pltpu....]
where the time goes in v4:
time: 26.9 us; the launch traced here: 26.7 us
  Pallas kernels  25.9 us (96%)
  local copies, waits for them, and re-layouts  0.8 us (3%)
    pallas_call x1, Pallas kernels, local(): pl.pallas_call(functools.partial(kernel, tasks, groups), out_shape=pltpu....  25.9 us
    unnamed x1, local copies, waits for them, and re-layouts  0.8 us

profile of v4, /device:TPU:0, one launch (start us, length us, event | category | flops | bytes accessed | tf_op | source)
XLA Modules:
  0.0 26.7 jit_solution(6776498659175363961)
XLA Ops:
  0.0 25.9 %merge.1 = bf16[64,4096]{1,0:T(8,128)(2,1)S(1)} custom-call(bf16[4,64,4096]{2,1,0:T(8,128)(2,1)} %params_hbm.1, f32[4,64,4096]{2,1,0:T(8,128)} %fisher_hbm.1), custom_call_target="tpu_custom_call" | custom-call | tf_op jit(solution)/shard_map/merge/pallas_call | solution.py:246
  26.0 0.8 %copy.4 = bf16[64,4096]{1,0:T(8,128)(2,1)} copy(bf16[64,4096]{1,0:T(8,128)(2,1)S(1)} %merge.1) | data formatting | bytes 1048576

commit v5 on v4

--- a/solution.py
+++ b/solution.py
@@ -10,6 +10,7 @@
 MESH = pl.DeviceIdType.MESH
 LANES = 128
 PIECES = 8
+AHEAD = 3
 
 
 def split(value):
@@ -59,7 +60,12 @@
     def drain(ref, semaphore):
         pltpu.make_async_copy(ref, ref, semaphore).wait()
 
-    loads_f = [pltpu.make_async_copy(fisher_hbm.at[t], fisher.at[t], load_f.at[t]) for t in range(count)]
+    spans = [(t, 0, width) for t in range(count - 1)] + [(count - 1, 0, half), (count - 1, half, half)]
+    loads_f = [
+        pltpu.make_async_copy(
+            fisher_hbm.at[t, :, pl.ds(start, size)], fisher.at[t, :, pl.ds(start, size)], load_f.at[n])
+        for n, (t, start, size) in enumerate(spans)
+    ]
     loads_p = [pltpu.make_async_copy(params_hbm.at[t], params.at[t], load_p) for t in range(count)]
     for copy in loads_f:
         copy.start()
@@ -72,9 +78,9 @@
         pl.semaphore_signal(barrier, inc=1, device_id=device, device_id_type=MESH)
 
     tops, sums = [], []
-    for t in range(count):
-        loads_f[t].wait()
-        if t == count - 1:
+    for n, (t, start, size) in enumerate(spans):
+        loads_f[n].wait()
+        if n == count:
             for copy in loads_p:
                 copy.start()
 
@@ -82,10 +88,14 @@
             block = fisher[t, :, pl.ds(pl.multiple_of(step * LANES, LANES), LANES)]
             return jnp.maximum(carry[0], block), carry[1] + block
 
-        first = fisher[t, :, 0:LANES]
-        top, total = lax.fori_loop(1, width // LANES, over, (first, first), unroll=8)
-        tops.append(jnp.max(top, axis=0, keepdims=True))
-        sums.append(jnp.sum(total, axis=0, keepdims=True))
+        begin = start // LANES
+        if start == 0:
+            first = fisher[t, :, 0:LANES]
+            top, total, begin = first, first, 1
+        top, total = lax.fori_loop(begin, (start + size) // LANES, over, (top, total), unroll=8)
+        if start + size == width:
+            tops.append(jnp.max(top, axis=0, keepdims=True))
+            sums.append(jnp.sum(total, axis=0, keepdims=True))
     top = jnp.max(jnp.concatenate(tops, axis=0), axis=1, keepdims=True)
     total = jnp.sum(jnp.concatenate(sums, axis=0), axis=1, keepdims=True)
     both = jnp.broadcast_to(jnp.concatenate([top, total], axis=0), (2 * count, LANES))
@@ -183,16 +193,18 @@
         gives[shift, k] = give_copy(shift, k)
         gives[shift, k].start()
 
-    for shift, k in away:
+    for shift, k in away[:AHEAD]:
         hand_over(shift, k)
     y_copies = {}
-    for shift, k in away:
+    for n, (shift, k) in enumerate(away):
         own = partial(core, chip_at(shift), k)
         gives[shift, k].wait_recv()
         wide_out[shift - 1, k], top_out[shift - 1, k] = coded(*added(own, take.at[shift, 0, k]))
         y_copies[shift, k] = y_copy(shift, k)
         for copy in y_copies[shift, k]:
             copy.start()
+        if n + AHEAD < len(away):
+            hand_over(*away[n + AHEAD])
     for k in range(chunks):
         hand_over(0, k)
     for k in range(chunks):
@@ -259,7 +271,7 @@
             pltpu.VMEM((far, chunks, rows, chunk), jnp.bfloat16),
             pltpu.VMEM((far, chunks, rows, chunk), f32),
             pltpu.VMEM((far, chunks, rows, chunk), jnp.bfloat16),
-            dma((count,)),
+            dma((count + 1,)),
             dma,
             dma,
             dma,

time: 26.9 us -> 26.4 us (0.981)
  Pallas kernels: 25.9 us -> 25.5 us
    pallas_call x1, Pallas kernels: 25.9 us -> 25.5 us  [local(): pl.pallas_call(functools.partial(kernel, tasks, groups), out_shape=pltpu....]
where the time goes in v5:
time: 26.4 us; the launch traced here: 26.3 us
  Pallas kernels  25.5 us (97%)
  local copies, waits for them, and re-layouts  0.8 us (3%)
    pallas_call x1, Pallas kernels, local(): pl.pallas_call(functools.partial(kernel, tasks, groups), out_shape=pltpu....  25.5 us
    unnamed x1, local copies, waits for them, and re-layouts  0.8 us

profile of v5, /device:TPU:0, one launch (start us, length us, event | category | flops | bytes accessed | tf_op | source)
XLA Modules:
  0.0 26.3 jit_solution(13467052763946956563)
XLA Ops:
  0.0 25.5 %merge.1 = bf16[64,4096]{1,0:T(8,128)(2,1)S(1)} custom-call(bf16[4,64,4096]{2,1,0:T(8,128)(2,1)} %params_hbm.1, f32[4,64,4096]{2,1,0:T(8,128)} %fisher_hbm.1), custom_call_target="tpu_custom_call" | custom-call | tf_op jit(solution)/shard_map/merge/pallas_call | solution.py:258
  25.5 0.8 %copy.4 = bf16[64,4096]{1,0:T(8,128)(2,1)} copy(bf16[64,4096]{1,0:T(8,128)(2,1)S(1)} %merge.1) | data formatting | bytes 1048576
